TPU v7x, 256 devices: a whole 4x4x8 slice. The times are simulated.
256 devices in a mesh: tm: 32 (over z, x_hi, core), rows: 8 (over x_lo, y).
Axes of the slice: x: 4 (x_hi: 2, x_lo: 2; x = x_hi * 2 + x_lo), y: 4, z: 8, core: 2. Of those that a mesh axis runs over, the one named last changes fastest.
Arguments:
- frames: bfloat16 [64, 64, 128, 128], P('tm', 'rows'), may hold values from -6 to 6
- conv_fine: bfloat16 [3, 3, 384, 128], replicated, may hold values from -0.109375 to 0.109375
- conv_down: bfloat16 [3, 384, 256], replicated, may hold values from -0.1875 to 0.1875
- conv_coarse: bfloat16 [3, 3, 768, 256], replicated, may hold values from -0.078125 to 0.078125
Outputs:
- coarse_out: bfloat16 [32, 32, 64, 256], P('tm', 'rows')
All inputs are finite; a program needn't handle non-finite values.
Results may differ from a plain program's by a relative error of at most 0.014.
Values may be sent and summed in bfloat16 or wider, within the bound.
A program may use at most 64 MiB of HBM per device.

v0:
```python
import jax
import jax.numpy as jnp
from jax import lax
from jax.sharding import PartitionSpec as P


def shifted(value, axis, steps):
    count = lax.axis_size(axis)
    first, last = (max(0, -steps), min(count, count - steps))
    return lax.ppermute(value, axis, [(source, source + steps) for source in range(first, last)])


def padded_2(cells, sides, width):
    for axis, dim in sides:
        count = lax.axis_size(axis)
        ends = count - 1
        head = lax.slice_in_dim(cells, 0, width, axis=dim)
        tail = lax.slice_in_dim(cells, cells.shape[dim] - width, cells.shape[dim], axis=dim)
        cells = jnp.concatenate(
            [
                lax.ppermute(tail, axis, [(i, (i + 1) % count) for i in range(ends)]),
                cells,
                lax.ppermute(head, axis, [((i + 1) % count, i) for i in range(ends)]),
            ],
            axis=dim,
        )
    return cells


def conv_block(extended, weight, frames_out, rows_out):
    col_count = extended.shape[2]
    channels = extended.shape[3]
    padded = jnp.pad(extended, ((0, 0), (0, 0), (1, 1), (0, 0)))
    stacked = jnp.concatenate(
        [
            padded[:, :, 0:col_count],
            padded[:, :, 1 : col_count + 1],
            padded[:, :, 2 : col_count + 2],
        ],
        axis=3,
    )
    total = jnp.zeros((frames_out * rows_out * col_count, weight.shape[-1]), jnp.float32)
    for time_tap in range(3):
        for row_tap in range(3):
            window = stacked[
                time_tap : time_tap + frames_out, row_tap : row_tap + rows_out
            ].reshape(-1, 3 * channels)
            total = total + jnp.dot(
                window, weight[time_tap, row_tap], preferred_element_type=jnp.float32
            )
    return total


def local(frames, conv_fine, conv_down, conv_coarse):
    frame_count, rows_dev, col_count, channels = frames.shape
    earlier = shifted(frames, "tm", 1)
    joined = jnp.concatenate([earlier, frames], axis=0)
    extended = padded_2(joined, (("rows", 1),), 1)
    total = conv_block(extended, conv_fine, frame_count, rows_dev)
    fine_out = (
        jax.nn.silu(total).astype(jnp.bfloat16).reshape(frame_count, rows_dev, col_count, channels)
    )
    widened = fine_out.astype(jnp.float32)
    pooled = ((widened[0] + widened[1]) * 0.5).astype(jnp.bfloat16)
    edge_row = shifted(pooled[0:1], "rows", -1)
    with_rim = jnp.concatenate([pooled, edge_row], axis=0)
    with_rim = jnp.pad(with_rim, ((0, 0), (0, 1), (0, 0)))
    half_rows = rows_dev // 2
    half_cols = col_count // 2
    stacked = jnp.concatenate(
        [with_rim[:, col_tap : col_tap + col_count : 2] for col_tap in range(3)], axis=2
    )
    down_total = jnp.zeros((half_rows * half_cols, conv_down.shape[-1]), jnp.float32)
    for row_tap in range(3):
        window = stacked[row_tap : row_tap + rows_dev : 2].reshape(-1, 3 * channels)
        down_total = down_total + jnp.dot(
            window, conv_down[row_tap], preferred_element_type=jnp.float32
        )
    reduced = down_total.astype(jnp.bfloat16).reshape(1, half_rows, half_cols, -1)
    carried = reduced
    history = [reduced]
    for repeat in range(2):
        carried = shifted(carried, "tm", 1)
        history.insert(0, carried)
    coarse_joined = jnp.concatenate(history, axis=0)
    coarse_extended = padded_2(coarse_joined, (("rows", 1),), 1)
    coarse_total = conv_block(coarse_extended, conv_coarse, 1, half_rows)
    return jax.nn.silu(coarse_total).astype(jnp.bfloat16).reshape(1, half_rows, half_cols, -1)


def solution(mesh):
    placed = (P("tm", "rows", None, None), P(), P(), P())
    return jax.shard_map(
        local, mesh=mesh, in_specs=placed, out_specs=P("tm", "rows", None, None), check_vma=False
    )
```

profile of v0, /device:TPU:152, one launch (start us, length us, event | category | flops | bytes accessed | tf_op | source)
XLA Modules:
  0.0 84.7 jit_solution(4313973126828041379)
XLA Ops:
  0.0 1.9 %collective-permute-start = (bf16[2,8,128,128]{3,2,1,0:T(8,128)(2,1)}, bf16[2,8,128,128]{3,2,1,0:T(8,128)(2,1)S(1)}, u32[]{:S(2)}, u32[]{:S(2)}) collective-permute-start(bf16[2,8,128,128]{3,2,1,0:T(8,128)(2,1)} %param.4), channel_id=1, source_target_pairs={{0,8},{8,16},{16,24},{24,32},{32,40},{40,48},{48,56},{56,64},{64,7... | collective-permute-start | bytes 1572872 | tf_op jit(solution)/shard_map/ppermute | solution.py:10
  1.9 12.4 %collective-permute-done = bf16[2,8,128,128]{3,2,1,0:T(8,128)(2,1)S(1)} collective-permute-done((bf16[2,8,128,128]{3,2,1,0:T(8,128)(2,1)}, bf16[2,8,128,128]{3,2,1,0:T(8,128)(2,1)S(1)}, u32[]{:S(2)}, u32[]{:S(2)}) %collective-permute-start) | collective-permute-done | bytes 524320 | tf_op jit(solution)/shard_map/ppermute | solution.py:10
  14.4 1.1 %constant_dynamic-update-slice_fusion = bf16[4,8,128,128]{3,2,1,0:T(8,128)(2,1)S(1)} fusion(bf16[4,8,128,128]{3,2,1,0:T(8,128)(2,1)S(1)} %constant_dynamic-update-slice_fusion.1, bf16[2,8,128,128]{3,2,1,0:T(8,128)(2,1)} %param.4), kind=kLoop, calls=%fused_computation.113 | loop fusion | bytes 1048576 | tf_op jit(solution)/shard_map/concatenate | solution.py:57
  15.5 3.1 %collective-permute-start.1 = (bf16[4,1,128,128]{3,2,1,0:T(8,128)(2,1)S(1)}, bf16[4,1,128,128]{3,2,1,0:T(8,128)(2,1)S(1)}, u32[]{:S(2)}, u32[]{:S(2)}) collective-permute-start(bf16[4,1,128,128]{3,2,1,0:T(8,128)(2,1)S(1)} %get-tuple-element.25), channel_id=1, source_target_pairs={{0,1},{1,2},{2,3},{3,4},{4,5},{5,6},{6,7},{8,9},{9,10},{10,11},{11... | collective-permute-start | bytes 393224 | tf_op jit(solution)/shard_map/ppermute | solution.py:21
  18.6 2.8 %collective-permute-start.2 = (bf16[4,1,128,128]{3,2,1,0:T(8,128)(2,1)S(1)}, bf16[4,1,128,128]{3,2,1,0:T(8,128)(2,1)S(1)}, u32[]{:S(2)}, u32[]{:S(2)}) collective-permute-start(bf16[4,1,128,128]{3,2,1,0:T(8,128)(2,1)S(1)} %get-tuple-element.26), channel_id=1, source_target_pairs={{1,0},{2,1},{3,2},{4,3},{5,4},{6,5},{7,6},{9,8},{10,9},{11,10},{12... | collective-permute-start | bytes 393224 | tf_op jit(solution)/shard_map/ppermute | solution.py:23
  21.4 1.0 %collective-permute-done.1 = bf16[4,1,128,128]{3,2,1,0:T(8,128)(2,1)S(1)} collective-permute-done((bf16[4,1,128,128]{3,2,1,0:T(8,128)(2,1)S(1)}, bf16[4,1,128,128]{3,2,1,0:T(8,128)(2,1)S(1)}, u32[]{:S(2)}, u32[]{:S(2)}) %collective-permute-start.1) | collective-permute-done | bytes 131104 | tf_op jit(solution)/shard_map/ppermute | solution.py:21
  22.4 5.2 %collective-permute-done.2 = bf16[4,1,128,128]{3,2,1,0:T(8,128)(2,1)S(1)} collective-permute-done((bf16[4,1,128,128]{3,2,1,0:T(8,128)(2,1)S(1)}, bf16[4,1,128,128]{3,2,1,0:T(8,128)(2,1)S(1)}, u32[]{:S(2)}, u32[]{:S(2)}) %collective-permute-start.2) | collective-permute-done | bytes 131104 | tf_op jit(solution)/shard_map/ppermute | solution.py:23
  27.6 0.6 fusion.12
  28.2 0.9 %fusion.96 = (bf16[4,10,128,128]{3,2,1,0:T(8,128)(2,1)S(1)}, bf16[4,10,128,128]{3,2,1,0:T(8,128)(2,1)S(1)}) fusion(bf16[4,10,130,128]{3,2,1,0:T(8,128)(2,1)S(1)} %fusion.12), kind=kLoop, calls=%fused_computation.117 | loop fusion | bytes 5242880 | tf_op jit(solution)/shard_map/slice | solution.py:36
  29.1 0.7 pad_maximum_fusion
  29.8 0.0 copy-start.1
  29.8 2.7 %fusion.94 = (bf16[2,8,128,384]{3,2,1,0:T(8,128)(2,1)S(1)}, bf16[2,8,128,384]{3,2,1,0:T(8,128)(2,1)S(1)}, bf16[2,8,128,384]{3,2,1,0:T(8,128)(2,1)S(1)}, bf16[2,8...) fusion(bf16[4,10,128,384]{3,2,1,0:T(8,128)(2,1)S(1)} %pad_maxim, ...), kind=kLoop, calls=%fused_computation.115 | loop fusion | bytes 28311552 | tf_op jit(solution)/shard_map/slice | solution.py:45
  32.5 0.0 copy-done.1
  32.5 0.6 fusion.68
  33.1 0.6 fusion.70
  33.7 0.6 fusion.72
  34.3 0.6 fusion.74
  34.8 0.6 fusion.76
  35.4 0.6 fusion.78
  36.0 0.6 fusion.80
  36.6 0.6 fusion.82
  37.1 0.9 %fusion.22 = f32[2048,128]{1,0:T(8,128)S(1)} fusion(f32[2048,128]{1,0:T(8,128)S(1)} %fusion.68, f32[2048,128]{1,0:T(8,128)S(1)} %fusion.70, f32[2048,128]{1,0:T(8,128)S(1)} %fusion.72, f32[2048,128]{1,0:T(8,128)S(1)} %fusion.74, f32[2048,128]{1,0:T(8,128)S(1)} %fusion.76, f32[2048,128]{1,0:T(8,128)S(1)} %fusion.78, f32[2048,128]{1,0:T(8,128)S(1)} %fusion.80, ...), kind=kOutput, calls=%fused_computation.33 | convolution fusion | flops 204996608 | bytes 11108352 | tf_op jit(solution)/shard_map/dot_general | solution.py:48
  38.1 0.1 fusion.31
  38.1 1.9 %collective-permute-start.3 = (bf16[1,128,128]{2,1,0:T(8,128)(2,1)S(1)}, bf16[1,128,128]{2,1,0:T(8,128)(2,1)S(1)}, u32[]{:S(2)}, u32[]{:S(2)}) collective-permute-start(bf16[1,128,128]{2,1,0:T(8,128)(2,1)S(1)} %slice_bitcast_fusion), channel_id=1, source_target_pairs={{1,0},{2,1},{3,2},{4,3},{5,4},{6,5},{7,6},{9,8},{10,9},{11,10},{12... | collective-permute-start | bytes 98312 | tf_op jit(solution)/shard_map/ppermute | solution.py:10
  40.1 6.0 %collective-permute-done.3 = bf16[1,128,128]{2,1,0:T(8,128)(2,1)S(1)} collective-permute-done((bf16[1,128,128]{2,1,0:T(8,128)(2,1)S(1)}, bf16[1,128,128]{2,1,0:T(8,128)(2,1)S(1)}, u32[]{:S(2)}, u32[]{:S(2)}) %collective-permute-start.3) | collective-permute-done | bytes 32800 | tf_op jit(solution)/shard_map/ppermute | solution.py:10
  46.1 0.0 copy-start.2
  46.1 0.3 slice.202
  46.5 0.3 slice.201
  46.8 0.5 slice.203
  47.3 0.1 pad_maximum_fusion.2
  47.4 0.1 fusion.99
  47.4 0.0 copy-done.2
  47.4 0.2 fusion.63
  47.7 0.2 convolution_add_fusion.3
  47.9 0.2 fusion.21
  48.1 1.9 %collective-permute-start.4 = (bf16[1,4,64,256]{3,2,1,0:T(8,128)(2,1)S(1)}, bf16[1,4,64,256]{3,2,1,0:T(8,128)(2,1)S(1)}, u32[]{:S(2)}, u32[]{:S(2)}) collective-permute-start(bf16[1,4,64,256]{3,2,1,0:T(8,128)(2,1)S(1)} %bitcast.122), channel_id=1, source_target_pairs={{0,8},{8,16},{16,24},{24,32},{32,40},{40,48},{48,56},{56,64},{64,7... | collective-permute-start | bytes 393224 | tf_op jit(solution)/shard_map/ppermute | solution.py:10
  50.1 8.0 %collective-permute-done.4 = bf16[1,4,64,256]{3,2,1,0:T(8,128)(2,1)S(1)} collective-permute-done((bf16[1,4,64,256]{3,2,1,0:T(8,128)(2,1)S(1)}, bf16[1,4,64,256]{3,2,1,0:T(8,128)(2,1)S(1)}, u32[]{:S(2)}, u32[]{:S(2)}) %collective-permute-start.4) | collective-permute-done | bytes 131104 | tf_op jit(solution)/shard_map/ppermute | solution.py:10
  58.0 1.9 %collective-permute-start.5 = (bf16[1,4,64,256]{3,2,1,0:T(8,128)(2,1)S(1)}, bf16[1,4,64,256]{3,2,1,0:T(8,128)(2,1)S(1)}, u32[]{:S(2)}, u32[]{:S(2)}) collective-permute-start(bf16[1,4,64,256]{3,2,1,0:T(8,128)(2,1)S(1)} %collective-permute-done.4), channel_id=1, source_target_pairs={{0,8},{8,16},{16,24},{24,32},{32,40},{40,48},{48,56},{56,64},{64,7... | collective-permute-start | bytes 393224 | tf_op jit(solution)/shard_map/ppermute | solution.py:10
  59.9 8.1 %collective-permute-done.5 = bf16[1,4,64,256]{3,2,1,0:T(8,128)(2,1)S(1)} collective-permute-done((bf16[1,4,64,256]{3,2,1,0:T(8,128)(2,1)S(1)}, bf16[1,4,64,256]{3,2,1,0:T(8,128)(2,1)S(1)}, u32[]{:S(2)}, u32[]{:S(2)}) %collective-permute-start.5) | collective-permute-done | bytes 131104 | tf_op jit(solution)/shard_map/ppermute | solution.py:10
  68.0 1.9 %collective-permute-start.6 = (bf16[3,1,64,256]{3,2,1,0:T(8,128)(2,1)S(1)}, bf16[3,1,64,256]{3,2,1,0:T(8,128)(2,1)S(1)}, u32[]{:S(2)}, u32[]{:S(2)}) collective-permute-start(bf16[3,1,64,256]{3,2,1,0:T(8,128)(2,1)S(1)} %get-tuple-element.32), channel_id=1, source_target_pairs={{0,1},{1,2},{2,3},{3,4},{4,5},{5,6},{6,7},{8,9},{9,10},{10,11},{11... | collective-permute-start | bytes 294920 | tf_op jit(solution)/shard_map/ppermute | solution.py:21
  70.0 3.9 %collective-permute-start.7 = (bf16[3,1,64,256]{3,2,1,0:T(8,128)(2,1)S(1)}, bf16[3,1,64,256]{3,2,1,0:T(8,128)(2,1)S(1)}, u32[]{:S(2)}, u32[]{:S(2)}) collective-permute-start(bf16[3,1,64,256]{3,2,1,0:T(8,128)(2,1)S(1)} %get-tuple-element.33), channel_id=1, source_target_pairs={{1,0},{2,1},{3,2},{4,3},{5,4},{6,5},{7,6},{9,8},{10,9},{11,10},{12... | collective-permute-start | bytes 294920 | tf_op jit(solution)/shard_map/ppermute | solution.py:23
  73.9 0.7 collective-permute-done.6
  74.6 4.0 %collective-permute-done.7 = bf16[3,1,64,256]{3,2,1,0:T(8,128)(2,1)S(1)} collective-permute-done((bf16[3,1,64,256]{3,2,1,0:T(8,128)(2,1)S(1)}, bf16[3,1,64,256]{3,2,1,0:T(8,128)(2,1)S(1)}, u32[]{:S(2)}, u32[]{:S(2)}) %collective-permute-start.7) | collective-permute-done | bytes 98336 | tf_op jit(solution)/shard_map/ppermute | solution.py:23
  78.6 0.3 select_maximum_fusion
  78.9 0.3 fusion.98
  79.2 0.2 pad_maximum_fusion.1
  79.4 0.0 copy-start
  79.4 0.4 fusion.95
  79.8 1.6 %copy-done = bf16[3,3,768,256]{3,2,1,0:T(8,128)(2,1)S(1)} copy-done((bf16[3,3,768,256]{3,2,1,0:T(8,128)(2,1)S(1)}, bf16[3,3,768,256]{3,2,1,0:T(8,128)(2,1)}, u32[]{:S(2)}) %copy-start) | copy-done | bytes 3538968
  81.4 0.3 fusion.32
  81.7 0.3 fusion.34
  82.0 0.3 fusion.36
  82.3 0.3 fusion.38
  82.5 0.3 fusion.40
  82.8 0.3 fusion.42
  83.1 0.3 fusion.44
  83.4 0.3 fusion.46
  83.6 1.0 %multiply_convert_fusion.1 = bf16[256,256]{1,0:T(8,128)(2,1)} fusion(f32[256,256]{1,0:T(8,128)S(1)} %fusion.32, f32[256,256]{1,0:T(8,128)S(1)} %fusion.34, f32[256,256]{1,0:T(8,128)S(1)} %fusion.36, f32[256,256]{1,0:T(8,128)S(1)} %fusion.38, f32[256,256]{1,0:T(8,128)S(1)} %fusion.40, f32[256,256]{1,0:T(8,128)S(1)} %fusion.42, f32[256,256]{1,0:T(8,128)S(1)} %fusion.44, ...), kind=kOutput, calls=%fused_computation.75 | convolution fusion | flops 101515264 | bytes 3014656 | tf_op jit(solution)/shard_map/dot_general | solution.py:48
  (5 shorter events, 0.1 us)
Async XLA Ops:
  0.0 14.3 %collective-permute-start = (bf16[2,8,128,128]{3,2,1,0:T(8,128)(2,1)}, bf16[2,8,128,128]{3,2,1,0:T(8,128)(2,1)S(1)}, u32[]{:S(2)}, u32[]{:S(2)}) collective-permute-start(bf16[2,8,128,128]{3,2,1,0:T(8,128)(2,1)} %param.4), channel_id=1, source_target_pairs={{0,8},{8,16},{16,24},{24,32},{32,40},{40,48},{48,56},{56,64},{64,7... | collective-permute-start | bytes 1572872 | tf_op jit(solution)/shard_map/ppermute | solution.py:10
  15.5 6.9 %collective-permute-start.1 = (bf16[4,1,128,128]{3,2,1,0:T(8,128)(2,1)S(1)}, bf16[4,1,128,128]{3,2,1,0:T(8,128)(2,1)S(1)}, u32[]{:S(2)}, u32[]{:S(2)}) collective-permute-start(bf16[4,1,128,128]{3,2,1,0:T(8,128)(2,1)S(1)} %get-tuple-element.25), channel_id=1, source_target_pairs={{0,1},{1,2},{2,3},{3,4},{4,5},{5,6},{6,7},{8,9},{9,10},{10,11},{11... | collective-permute-start | bytes 393224 | tf_op jit(solution)/shard_map/ppermute | solution.py:21
  18.6 9.0 %collective-permute-start.2 = (bf16[4,1,128,128]{3,2,1,0:T(8,128)(2,1)S(1)}, bf16[4,1,128,128]{3,2,1,0:T(8,128)(2,1)S(1)}, u32[]{:S(2)}, u32[]{:S(2)}) collective-permute-start(bf16[4,1,128,128]{3,2,1,0:T(8,128)(2,1)S(1)} %get-tuple-element.26), channel_id=1, source_target_pairs={{1,0},{2,1},{3,2},{4,3},{5,4},{6,5},{7,6},{9,8},{10,9},{11,10},{12... | collective-permute-start | bytes 393224 | tf_op jit(solution)/shard_map/ppermute | solution.py:23
  29.8 2.8 %copy-start.1 = (bf16[3,3,384,128]{3,2,1,0:T(8,128)(2,1)S(1)}, bf16[3,3,384,128]{3,2,1,0:T(8,128)(2,1)}, u32[]{:S(2)}) copy-start(bf16[3,3,384,128]{3,2,1,0:T(8,128)(2,1)} %param.5) | copy-start | bytes 2654212
  38.1 7.9 %collective-permute-start.3 = (bf16[1,128,128]{2,1,0:T(8,128)(2,1)S(1)}, bf16[1,128,128]{2,1,0:T(8,128)(2,1)S(1)}, u32[]{:S(2)}, u32[]{:S(2)}) collective-permute-start(bf16[1,128,128]{2,1,0:T(8,128)(2,1)S(1)} %slice_bitcast_fusion), channel_id=1, source_target_pairs={{1,0},{2,1},{3,2},{4,3},{5,4},{6,5},{7,6},{9,8},{10,9},{11,10},{12... | collective-permute-start | bytes 98312 | tf_op jit(solution)/shard_map/ppermute | solution.py:10
  46.1 1.3 %copy-start.2 = (bf16[3,384,256]{2,1,0:T(8,128)(2,1)S(1)}, bf16[3,384,256]{2,1,0:T(8,128)(2,1)}, u32[]{:S(2)}) copy-start(bf16[3,384,256]{2,1,0:T(8,128)(2,1)} %param.6) | copy-start | bytes 1769476
  48.1 9.9 %collective-permute-start.4 = (bf16[1,4,64,256]{3,2,1,0:T(8,128)(2,1)S(1)}, bf16[1,4,64,256]{3,2,1,0:T(8,128)(2,1)S(1)}, u32[]{:S(2)}, u32[]{:S(2)}) collective-permute-start(bf16[1,4,64,256]{3,2,1,0:T(8,128)(2,1)S(1)} %bitcast.122), channel_id=1, source_target_pairs={{0,8},{8,16},{16,24},{24,32},{32,40},{40,48},{48,56},{56,64},{64,7... | collective-permute-start | bytes 393224 | tf_op jit(solution)/shard_map/ppermute | solution.py:10
  58.0 10.0 %collective-permute-start.5 = (bf16[1,4,64,256]{3,2,1,0:T(8,128)(2,1)S(1)}, bf16[1,4,64,256]{3,2,1,0:T(8,128)(2,1)S(1)}, u32[]{:S(2)}, u32[]{:S(2)}) collective-permute-start(bf16[1,4,64,256]{3,2,1,0:T(8,128)(2,1)S(1)} %collective-permute-done.4), channel_id=1, source_target_pairs={{0,8},{8,16},{16,24},{24,32},{32,40},{40,48},{48,56},{56,64},{64,7... | collective-permute-start | bytes 393224 | tf_op jit(solution)/shard_map/ppermute | solution.py:10
  68.0 6.5 %collective-permute-start.6 = (bf16[3,1,64,256]{3,2,1,0:T(8,128)(2,1)S(1)}, bf16[3,1,64,256]{3,2,1,0:T(8,128)(2,1)S(1)}, u32[]{:S(2)}, u32[]{:S(2)}) collective-permute-start(bf16[3,1,64,256]{3,2,1,0:T(8,128)(2,1)S(1)} %get-tuple-element.32), channel_id=1, source_target_pairs={{0,1},{1,2},{2,3},{3,4},{4,5},{5,6},{6,7},{8,9},{9,10},{10,11},{11... | collective-permute-start | bytes 294920 | tf_op jit(solution)/shard_map/ppermute | solution.py:21
  70.0 8.6 %collective-permute-start.7 = (bf16[3,1,64,256]{3,2,1,0:T(8,128)(2,1)S(1)}, bf16[3,1,64,256]{3,2,1,0:T(8,128)(2,1)S(1)}, u32[]{:S(2)}, u32[]{:S(2)}) collective-permute-start(bf16[3,1,64,256]{3,2,1,0:T(8,128)(2,1)S(1)} %get-tuple-element.33), channel_id=1, source_target_pairs={{1,0},{2,1},{3,2},{4,3},{5,4},{6,5},{7,6},{9,8},{10,9},{11,10},{12... | collective-permute-start | bytes 294920 | tf_op jit(solution)/shard_map/ppermute | solution.py:23
  79.4 2.0 %copy-start = (bf16[3,3,768,256]{3,2,1,0:T(8,128)(2,1)S(1)}, bf16[3,3,768,256]{3,2,1,0:T(8,128)(2,1)}, u32[]{:S(2)}) copy-start(bf16[3,3,768,256]{3,2,1,0:T(8,128)(2,1)} %param.7) | copy-start | bytes 10616836
where the time goes:
time: 85 us; the launch traced here: 84.7 us
  waiting for transfers between devices  45.3 us (53%)
  starting transfers between devices  19.3 us (23%)
  matrix products  9.3 us (11%)
  local copies, waits for them, and re-layouts  8.39 us (10%)
  other arithmetic  1.92 us (2%)
    ppermute x4, waiting for transfers between devices, shifted(): lax.ppermute(value, axis, [(source, source + steps) for source in range(f...  34.4 us
    ppermute x2, waiting for transfers between devices, padded_2(): lax.ppermute(head, axis, [((i + 1) % count, i) for i in range(ends)])  9.21 us
    dot_general x18, matrix products, conv_block(): jnp.dot(window, weight[time_tap, row_tap], preferred_element_type=jnp.flo...  8.64 us
    ppermute x4, starting transfers between devices, shifted(): lax.ppermute(value, axis, [(source, source + steps) for source in range(f...  7.66 us
    ppermute x2, starting transfers between devices, padded_2(): lax.ppermute(head, axis, [((i + 1) % count, i) for i in range(ends)])  6.71 us
    ppermute x2, starting transfers between devices, padded_2(): lax.ppermute(tail, axis, [(i, (i + 1) % count) for i in range(ends)])  4.98 us
    slice x2, local copies, waits for them, and re-layouts, conv_block(): stacked[time_tap:time_tap + frames_out, row_tap:row_tap + rows_out]  3.16 us
  transfers between devices with their start and end apart: 8, of which 8 were waited for; matrix products, arithmetic and copies ran while one was open for 0% of the time, Pallas kernels for 0%

commit v1 on v0

v1 whole, which is shorter than its diff:
```python
import jax
import jax.numpy as jnp
from jax import lax
from jax.experimental import pallas as pl
from jax.experimental.pallas import tpu as pltpu
from jax.sharding import PartitionSpec as P

MESH = pl.DeviceIdType.MESH
F32 = jnp.float32
BF16 = jnp.bfloat16

E0, E1, M0, M1, OU, OD, FU, FD, PR = range(9)
N1A, N1B, N2A, N2B, T2U, T2D, T1U, T1D, T0U, T0D = range(9, 19)
HA, HB, S0, S1 = 19, 20, 21, 22
COPIES = 23


def silu(v):
    return v / (1.0 + jnp.exp(-v))


def spread(y0, y1, y2, cols):
    col = lax.broadcasted_iota(jnp.int32, y0.shape, 0) % cols
    left = jnp.where(col == 0, 0.0, pltpu.roll(y0, 1, 0))
    right = jnp.where(col == cols - 1, 0.0, pltpu.roll(y2, y2.shape[0] - 1, 0))
    return left + y1 + right


def dot(a, b):
    return jnp.dot(a, b, preferred_element_type=F32)


def kernel(
    tms, rws, frames, wf_h, wd_h, wc_h, out, x, wf, wd, wc, z, pool, red, y, ssem, rsem, lsem
):
    tm = lax.axis_index("tm")
    row = lax.axis_index("rows")
    core = tm % 2
    has_next, has_prev = tm < tms - 1, tm > 0
    has_prev2 = tm > 1
    up, down = row > 0, row < rws - 1
    first = core == 0
    hop2 = first & (tm < tms - 2)
    from2 = first & has_prev2

    barrier = pltpu.get_barrier_semaphore()
    total = jnp.int32(0)
    for ok, dev in (
        (has_next, (tm + 1, row)),
        (has_prev, (tm - 1, row)),
        (up, (tm, row - 1)),
        (down, (tm, row + 1)),
        (hop2, (tm + 2, row)),
        (from2, (tm - 2, row)),
    ):

        @pl.when(ok)
        def _():
            pl.semaphore_signal(barrier, inc=1, device_id=dev, device_id_type=MESH)

        total = total + ok.astype(jnp.int32)

    loads = [
        pltpu.make_async_copy(frames, x.at[pl.ds(2, 2), pl.ds(1, 8)], lsem.at[0]),
        pltpu.make_async_copy(wf_h, wf, lsem.at[1]),
        pltpu.make_async_copy(wd_h, wd, lsem.at[2]),
        pltpu.make_async_copy(wc_h, wc, lsem.at[3]),
    ]
    for load in loads:
        load.start()

    pool[:, pl.ds(128, 8), :] = jnp.zeros((9, 8, 128), F32)

    @pl.when(~up)
    def _():
        x[:, 0] = jnp.zeros((4, 128, 128), BF16)
        red[:, 0] = jnp.zeros((3, 64, 256), BF16)

    @pl.when(~down)
    def _():
        x[:, 9] = jnp.zeros((4, 128, 128), BF16)
        red[:, 5] = jnp.zeros((3, 64, 256), BF16)
        pool[8, pl.ds(0, 128)] = jnp.zeros((128, 128), F32)

    @pl.when(~has_prev)
    def _():
        x[0:2, pl.ds(1, 8)] = jnp.zeros((2, 8, 128, 128), BF16)
        red[1, pl.ds(1, 4)] = jnp.zeros((4, 64, 256), BF16)

        @pl.when(up)
        def _():
            x[0:2, 0] = jnp.zeros((2, 128, 128), BF16)
            red[1, 0] = jnp.zeros((64, 256), BF16)

        @pl.when(down)
        def _():
            x[0:2, 9] = jnp.zeros((2, 128, 128), BF16)
            red[1, 5] = jnp.zeros((64, 256), BF16)

    @pl.when(~has_prev2)
    def _():
        red[0, pl.ds(1, 4)] = jnp.zeros((4, 64, 256), BF16)

        @pl.when(up)
        def _():
            red[0, 0] = jnp.zeros((64, 256), BF16)

        @pl.when(down)
        def _():
            red[0, 5] = jnp.zeros((64, 256), BF16)

    def remote(k, src, dst, dev, recv=None):
        return pltpu.make_async_remote_copy(
            src_ref=src,
            dst_ref=dst,
            send_sem=ssem.at[k],
            recv_sem=rsem.at[k if recv is None else recv],
            device_id=dev,
            device_id_type=MESH,
        )

    sent = []

    def send(ok, copy):
        @pl.when(ok)
        def _():
            copy.start()

        sent.append((ok, copy))

    def arrived(ok, copy):
        @pl.when(ok)
        def _():
            copy.wait_recv()

    nxt, nx2 = (tm + 1, row), (tm + 2, row)
    above, below = (tm, row - 1), (tm, row + 1)
    own, old = pl.ds(2, 2), pl.ds(0, 2)
    c = {
        E0: remote(E0, x.at[own, pl.ds(1, 1)], x.at[old, pl.ds(1, 1)], nxt),
        E1: remote(E1, x.at[own, pl.ds(8, 1)], x.at[old, pl.ds(8, 1)], nxt),
        S0: remote(S0, x.at[own, pl.ds(2, 1)], x.at[old, pl.ds(2, 1)], nxt),
        S1: remote(S1, x.at[own, pl.ds(7, 1)], x.at[old, pl.ds(7, 1)], nxt),
        M0: remote(M0, x.at[own, pl.ds(3, 2)], x.at[old, pl.ds(3, 2)], nxt),
        M1: remote(M1, x.at[own, pl.ds(5, 2)], x.at[old, pl.ds(5, 2)], nxt),
        OU: remote(OU, x.at[own, pl.ds(1, 1)], x.at[own, pl.ds(9, 1)], above),
        OD: remote(OD, x.at[own, pl.ds(8, 1)], x.at[own, pl.ds(0, 1)], below),
        FU: remote(FU, x.at[old, pl.ds(1, 1)], x.at[old, pl.ds(9, 1)], above),
        FD: remote(FD, x.at[old, pl.ds(8, 1)], x.at[old, pl.ds(0, 1)], below),
        PR: remote(PR, pool.at[0, pl.ds(0, 128)], pool.at[8, pl.ds(0, 128)], above),
        N1A: remote(N1A, red.at[2, pl.ds(1, 3)], red.at[1, pl.ds(1, 3)], nxt),
        N1B: remote(N1B, red.at[2, pl.ds(4, 1)], red.at[1, pl.ds(4, 1)], nxt),
        T2U: remote(T2U, red.at[2, pl.ds(1, 1)], red.at[2, pl.ds(5, 1)], above),
        T2D: remote(T2D, red.at[2, pl.ds(4, 1)], red.at[2, pl.ds(0, 1)], below),
        T1U: remote(T1U, red.at[1, pl.ds(1, 1)], red.at[1, pl.ds(5, 1)], above),
        T1D: remote(T1D, red.at[1, pl.ds(4, 1)], red.at[1, pl.ds(0, 1)], below),
        T0U: remote(T0U, red.at[0, pl.ds(1, 1)], red.at[0, pl.ds(5, 1)], above),
        T0D: remote(T0D, red.at[0, pl.ds(4, 1)], red.at[0, pl.ds(0, 1)], below),
    }
    far_a = remote(N2A, red.at[2, pl.ds(1, 3)], red.at[0, pl.ds(1, 3)], nx2)
    far_b = remote(N2B, red.at[2, pl.ds(4, 1)], red.at[0, pl.ds(4, 1)], nx2)
    hand_a = remote(HA, red.at[1, pl.ds(1, 3)], red.at[0, pl.ds(1, 3)], nxt, N2A)
    hand_b = remote(HB, red.at[1, pl.ds(4, 1)], red.at[0, pl.ds(4, 1)], nxt, N2B)

    def tap(a, b, e):
        return wf[a, b, pl.ds(e * 128, 128), :]

    def fine(lhs, main, side, both, single, other):
        left = jnp.concatenate(
            [lhs(main, b) for b in range(3)] + [lhs(side, b) for b in range(3)], axis=1
        )

        def rhs(pairs):
            return jnp.concatenate([jnp.concatenate(pair, axis=1) for pair in pairs], axis=0)

        none = jnp.zeros((128, 128), BF16)
        n0 = dot(
            left,
            rhs(
                [(tap(both, b, 0), tap(both, b, 1)) for b in range(3)]
                + [(tap(single, b, 0), tap(single, b, 1)) for b in range(3)]
            ),
        )
        n1 = dot(
            left,
            rhs(
                [(tap(both, b, 2), tap(other, b, 0)) for b in range(3)]
                + [(tap(single, b, 2), none) for b in range(3)]
            ),
        )
        n2 = dot(left[:, :384], rhs([(tap(other, b, 1), tap(other, b, 2)) for b in range(3)]))
        mine = spread(n0[:, :128], n0[:, 128:], n1[:, :128], 128)
        rest = spread(n1[:, 128:], n2[:, :128], n2[:, 128:], 128)
        return mine, rest

    def late(lhs):
        second, head = fine(lhs, 2, 3, 1, 2, 2)
        return head, second

    def early(lhs):
        return fine(lhs, 1, 0, 1, 0, 0)

    def pooled(head, second):
        a = silu(head).astype(BF16).astype(F32)
        b = silu(second).astype(BF16).astype(F32)
        return ((a + b) * 0.5).astype(BF16).astype(F32)

    def inner(r):
        return lambda f, b: x[f, pl.ds(r + b, 2)].reshape(256, 128)

    def edges(f, b):
        return jnp.concatenate([x[f, b], x[f, 7 + b]], axis=0)

    loads[0].wait()
    loads[1].wait()

    def own_part(i, carry):
        r = 2 * i + 1
        head, second = late(inner(r))
        z[0, pl.ds(r, 2)] = head.reshape(2, 128, 128)
        z[1, pl.ds(r, 2)] = second.reshape(2, 128, 128)
        return carry

    lax.fori_loop(0, 3, own_part, 0)
    pl.semaphore_wait(barrier, total)

    send(up, c[OU])
    send(down, c[OD])
    for k in (E0, E1, S0, S1, M0, M1):
        send(has_next, c[k])

    arrived(has_prev, c[E0])
    send(up & has_prev, c[FU])
    arrived(has_prev, c[E1])
    send(down & has_prev, c[FD])
    arrived(down, c[OU])
    arrived(up, c[OD])
    arrived(down & has_prev, c[FU])
    arrived(up & has_prev, c[FD])
    arrived(has_prev, c[S0])
    arrived(has_prev, c[S1])

    head_a, second_a = late(edges)
    head_b, second_b = early(edges)
    ends = pooled(head_a + head_b, second_a + second_b)
    pool[0, pl.ds(0, 128)] = ends[:128]
    pool[7, pl.ds(0, 128)] = ends[128:]
    send(up, c[PR])

    def rest_part(i, carry):
        r = 2 * i + 1
        head, second = early(inner(r))
        head = head + z[0, pl.ds(r, 2)].reshape(256, 128)
        second = second + z[1, pl.ds(r, 2)].reshape(256, 128)
        pool[pl.ds(r, 2), pl.ds(0, 128)] = pooled(head, second).reshape(2, 128, 128)
        return carry

    arrived(has_prev, c[M0])
    rest_part(0, 0)
    arrived(has_prev, c[M1])
    lax.fori_loop(1, 3, rest_part, 0)

    loads[2].wait()
    arrived(down, c[PR])
    weight = wd[...].reshape(1152, 256)
    strips = [
        jnp.concatenate(
            [
                pool[2 * p + b, pl.ds(e, 64, stride=2), :].astype(BF16)
                for b in range(3)
                for e in range(3)
            ],
            axis=1,
        )
        for p in range(4)
    ]
    red[2, pl.ds(1, 4)] = (
        dot(jnp.concatenate(strips, axis=0), weight).astype(BF16).reshape(4, 64, 256)
    )

    send(up, c[T2U])
    send(down, c[T2D])
    send(has_next, c[N1A])
    send(hop2, far_a)
    send(has_next, c[N1B])
    send(hop2, far_b)

    loads[3].wait()
    arrived(down, c[T2U])
    arrived(up, c[T2D])

    def coarse(a, e):
        left = jnp.concatenate(
            [red[a, pl.ds(b, 4)].reshape(256, 256) for b in range(3)], axis=1
        )
        right = jnp.concatenate([wc[a, b, pl.ds(e * 256, 256), :] for b in range(3)], axis=0)
        return dot(left, right)

    for e in range(3):
        y[e] = coarse(2, e)

    hand = first & has_prev
    arrived(has_prev, c[N1A])
    send(hand, hand_a)
    send(up & has_prev, c[T1U])
    arrived(has_prev, c[N1B])
    send(hand, hand_b)
    send(down & has_prev, c[T1D])
    arrived(has_prev2, far_a)
    send(up & has_prev2, c[T0U])
    arrived(has_prev2, far_b)
    send(down & has_prev2, c[T0D])
    arrived(down & has_prev, c[T1U])
    arrived(up & has_prev, c[T1D])
    for e in range(3):
        y[e] = y[e] + coarse(1, e)
    arrived(down & has_prev2, c[T0U])
    arrived(up & has_prev2, c[T0D])
    parts = [y[e] + coarse(0, e) for e in range(3)]
    out[...] = silu(spread(*parts, 64)).astype(BF16).reshape(1, 4, 64, 256)

    for ok, copy in sent:

        @pl.when(ok)
        def _():
            copy.wait_send()


def solution(mesh):
    import functools

    tms, rws = mesh.shape["tm"], mesh.shape["rows"]
    anywhere = pl.BlockSpec(memory_space=pl.ANY)

    def local(frames, conv_fine, conv_down, conv_coarse):
        return pl.pallas_call(
            functools.partial(kernel, tms, rws),
            out_shape=jax.ShapeDtypeStruct((1, 4, 64, 256), BF16),
            in_specs=[anywhere] * 4,
            out_specs=pl.BlockSpec(memory_space=pltpu.VMEM),
            scratch_shapes=[
                pltpu.VMEM((4, 10, 128, 128), BF16),
                pltpu.VMEM((3, 3, 384, 128), BF16),
                pltpu.VMEM((3, 384, 256), BF16),
                pltpu.VMEM((3, 3, 768, 256), BF16),
                pltpu.VMEM((2, 8, 128, 128), F32),
                pltpu.VMEM((9, 136, 128), F32),
                pltpu.VMEM((3, 6, 64, 256), BF16),
                pltpu.VMEM((3, 256, 256), F32),
                pltpu.SemaphoreType.DMA((COPIES,)),
                pltpu.SemaphoreType.DMA((COPIES,)),
                pltpu.SemaphoreType.DMA((4,)),
            ],
            compiler_params=pltpu.CompilerParams(
                collective_id=0, has_side_effects=True, vmem_limit_bytes=60 * 1024 * 1024
            ),
            name="encoder",
        )(frames, conv_fine, conv_down, conv_coarse)

    placed = (P("tm", "rows", None, None), P(), P(), P())
    return jax.shard_map(
        local, mesh=mesh, in_specs=placed, out_specs=P("tm", "rows", None, None), check_vma=False
    )
```

time: 85 us -> 37 us (0.44)
  the two profiles are of different devices: /device:TPU:152 before, /device:TPU:162 now
where the time goes in v1:
time: 37 us; the launch traced here: 36.9 us
  Pallas kernels  35.4 us (96%)
  local copies, waits for them, and re-layouts  1.57 us (4%)
    pallas_call x1, Pallas kernels, local(): pl.pallas_call(functools.partial(kernel, tms, rws), out_shape=jax.ShapeDt...  35.4 us
    unnamed x1, local copies, waits for them, and re-layouts  1.57 us

profile of v1, /device:TPU:162, one launch (start us, length us, event | category | flops | bytes accessed | tf_op | source)
XLA Modules:
  0.0 36.9 jit_solution(4828787537002357326)
XLA Ops:
  0.0 35.4 %encoder.1 = bf16[1,4,64,256]{3,2,1,0:T(8,128)(2,1)} custom-call(bf16[2,8,128,128]{3,2,1,0:T(8,128)(2,1)} %frames.1, bf16[3,3,384,128]{3,2,1,0:T(8,128)(2,1)} %wf_h.1, bf16[3,384,256]{2,1,0:T(8,128)(2,1)} %wd_h.1, bf16[3,3,768,256]{3,2,1,0:T(8,128)(2,1)} %wc_h.1), custom_call_target="tpu_custom_call" | custom-call | tf_op jit(solution)/shard_map/encoder/pallas_call | solution.py:336
  35.4 1.6 %copy.6 = bf16[1,4,64,256]{3,2,1,0:T(8,128)(2,1)} copy(bf16[1,4,64,256]{3,2,1,0:T(8,128)(2,1)} %encoder.1) | data formatting | bytes 262144

commit v2 on v1

--- a/solution.py
+++ b/solution.py
@@ -9,10 +9,12 @@
 F32 = jnp.float32
 BF16 = jnp.bfloat16
 
-E0, E1, M0, M1, OU, OD, FU, FD, PR = range(9)
-N1A, N1B, N2A, N2B, T2U, T2D, T1U, T1D, T0U, T0D = range(9, 19)
-HA, HB, S0, S1 = 19, 20, 21, 22
-COPIES = 23
+NAMES = (
+    "E0", "E1", "S0", "M0", "M1", "OU", "OD", "FU", "FD", "HU", "HD", "PR",
+    "NU", "ND", "NM", "QU", "QD", "QM", "GU", "GD", "GM", "T2U", "T2D", "T1U",
+    "T1D", "T0U", "T0D", "K1U", "K1D", "K0U", "K0D",
+)
+IDS = {name: i for i, name in enumerate(NAMES)}
 
 
 def silu(v):
@@ -31,17 +33,17 @@
 
 
 def kernel(
-    tms, rws, frames, wf_h, wd_h, wc_h, out, x, wf, wd, wc, z, pool, red, y, ssem, rsem, lsem
+    tms, rws, frames, wf_h, wd_h, wc_h, out, x, wf, wd, wc, z, pool, rim, red, y, ssem, rsem, lsem
 ):
     tm = lax.axis_index("tm")
     row = lax.axis_index("rows")
-    core = tm % 2
+    first = tm % 2 == 0
+    second = ~first
     has_next, has_prev = tm < tms - 1, tm > 0
-    has_prev2 = tm > 1
+    has_next2, has_prev2 = tm < tms - 2, tm > 1
     up, down = row > 0, row < rws - 1
-    first = core == 0
-    hop2 = first & (tm < tms - 2)
-    from2 = first & has_prev2
+    half = rws // 2
+    cross_up, cross_down = row == half, row == half - 1
 
     barrier = pltpu.get_barrier_semaphore()
     total = jnp.int32(0)
@@ -50,8 +52,16 @@
         (has_prev, (tm - 1, row)),
         (up, (tm, row - 1)),
         (down, (tm, row + 1)),
-        (hop2, (tm + 2, row)),
-        (from2, (tm - 2, row)),
+        (first & has_next2, (tm + 2, row)),
+        (first & has_prev2, (tm - 2, row)),
+        (second & has_next & cross_up, (tm + 1, row - 1)),
+        (second & has_next & cross_down, (tm + 1, row + 1)),
+        (first & has_prev & cross_up, (tm - 1, row - 1)),
+        (first & has_prev & cross_down, (tm - 1, row + 1)),
+        (first & has_next2 & cross_up, (tm + 2, row - 1)),
+        (first & has_next2 & cross_down, (tm + 2, row + 1)),
+        (first & has_prev2 & cross_up, (tm - 2, row - 1)),
+        (first & has_prev2 & cross_down, (tm - 2, row + 1)),
     ):
 
         @pl.when(ok)
@@ -80,7 +90,7 @@
     def _():
         x[:, 9] = jnp.zeros((4, 128, 128), BF16)
         red[:, 5] = jnp.zeros((3, 64, 256), BF16)
-        pool[8, pl.ds(0, 128)] = jnp.zeros((128, 128), F32)
+        rim[1] = jnp.zeros((128, 128), BF16)
 
     @pl.when(~has_prev)
     def _():
@@ -109,58 +119,49 @@
         def _():
             red[0, 5] = jnp.zeros((64, 256), BF16)
 
-    def remote(k, src, dst, dev, recv=None):
-        return pltpu.make_async_remote_copy(
+    sent = []
+
+    def send(ok, name, src, dst, dev, recv=None):
+        copy = pltpu.make_async_remote_copy(
             src_ref=src,
             dst_ref=dst,
-            send_sem=ssem.at[k],
-            recv_sem=rsem.at[k if recv is None else recv],
+            send_sem=ssem.at[IDS[name]],
+            recv_sem=rsem.at[IDS[recv or name]],
             device_id=dev,
             device_id_type=MESH,
         )
 
-    sent = []
-
-    def send(ok, copy):
         @pl.when(ok)
         def _():
             copy.start()
 
         sent.append((ok, copy))
 
-    def arrived(ok, copy):
+    def arrived(ok, name, dst):
+        copy = pltpu.make_async_remote_copy(
+            src_ref=dst,
+            dst_ref=dst,
+            send_sem=ssem.at[IDS[name]],
+            recv_sem=rsem.at[IDS[name]],
+            device_id=nxt,
+            device_id_type=MESH,
+        )
+
         @pl.when(ok)
         def _():
             copy.wait_recv()
 
     nxt, nx2 = (tm + 1, row), (tm + 2, row)
     above, below = (tm, row - 1), (tm, row + 1)
-    own, old = pl.ds(2, 2), pl.ds(0, 2)
-    c = {
-        E0: remote(E0, x.at[own, pl.ds(1, 1)], x.at[old, pl.ds(1, 1)], nxt),
-        E1: remote(E1, x.at[own, pl.ds(8, 1)], x.at[old, pl.ds(8, 1)], nxt),
-        S0: remote(S0, x.at[own, pl.ds(2, 1)], x.at[old, pl.ds(2, 1)], nxt),
-        S1: remote(S1, x.at[own, pl.ds(7, 1)], x.at[old, pl.ds(7, 1)], nxt),
-        M0: remote(M0, x.at[own, pl.ds(3, 2)], x.at[old, pl.ds(3, 2)], nxt),
-        M1: remote(M1, x.at[own, pl.ds(5, 2)], x.at[old, pl.ds(5, 2)], nxt),
-        OU: remote(OU, x.at[own, pl.ds(1, 1)], x.at[own, pl.ds(9, 1)], above),
-        OD: remote(OD, x.at[own, pl.ds(8, 1)], x.at[own, pl.ds(0, 1)], below),
-        FU: remote(FU, x.at[old, pl.ds(1, 1)], x.at[old, pl.ds(9, 1)], above),
-        FD: remote(FD, x.at[old, pl.ds(8, 1)], x.at[old, pl.ds(0, 1)], below),
-        PR: remote(PR, pool.at[0, pl.ds(0, 128)], pool.at[8, pl.ds(0, 128)], above),
-        N1A: remote(N1A, red.at[2, pl.ds(1, 3)], red.at[1, pl.ds(1, 3)], nxt),
-        N1B: remote(N1B, red.at[2, pl.ds(4, 1)], red.at[1, pl.ds(4, 1)], nxt),
-        T2U: remote(T2U, red.at[2, pl.ds(1, 1)], red.at[2, pl.ds(5, 1)], above),
-        T2D: remote(T2D, red.at[2, pl.ds(4, 1)], red.at[2, pl.ds(0, 1)], below),
-        T1U: remote(T1U, red.at[1, pl.ds(1, 1)], red.at[1, pl.ds(5, 1)], above),
-        T1D: remote(T1D, red.at[1, pl.ds(4, 1)], red.at[1, pl.ds(0, 1)], below),
-        T0U: remote(T0U, red.at[0, pl.ds(1, 1)], red.at[0, pl.ds(5, 1)], above),
-        T0D: remote(T0D, red.at[0, pl.ds(4, 1)], red.at[0, pl.ds(0, 1)], below),
-    }
-    far_a = remote(N2A, red.at[2, pl.ds(1, 3)], red.at[0, pl.ds(1, 3)], nx2)
-    far_b = remote(N2B, red.at[2, pl.ds(4, 1)], red.at[0, pl.ds(4, 1)], nx2)
-    hand_a = remote(HA, red.at[1, pl.ds(1, 3)], red.at[0, pl.ds(1, 3)], nxt, N2A)
-    hand_b = remote(HB, red.at[1, pl.ds(4, 1)], red.at[0, pl.ds(4, 1)], nxt, N2B)
+
+    def own(r, n=1):
+        return x.at[pl.ds(2, 2), pl.ds(r, n)]
+
+    def old(r, n=1):
+        return x.at[pl.ds(0, 2), pl.ds(r, n)]
+
+    def part(a, r, n=1):
+        return red.at[a, pl.ds(r, n)]
 
     def tap(a, b, e):
         return wf[a, b, pl.ds(e * 128, 128), :]
@@ -208,9 +209,6 @@
     def inner(r):
         return lambda f, b: x[f, pl.ds(r + b, 2)].reshape(256, 128)
 
-    def edges(f, b):
-        return jnp.concatenate([x[f, b], x[f, 7 + b]], axis=0)
-
     loads[0].wait()
     loads[1].wait()
 
@@ -224,28 +222,37 @@
     lax.fori_loop(0, 3, own_part, 0)
     pl.semaphore_wait(barrier, total)
 
-    send(up, c[OU])
-    send(down, c[OD])
-    for k in (E0, E1, S0, S1, M0, M1):
-        send(has_next, c[k])
-
-    arrived(has_prev, c[E0])
-    send(up & has_prev, c[FU])
-    arrived(has_prev, c[E1])
-    send(down & has_prev, c[FD])
-    arrived(down, c[OU])
-    arrived(up, c[OD])
-    arrived(down & has_prev, c[FU])
-    arrived(up & has_prev, c[FD])
-    arrived(has_prev, c[S0])
-    arrived(has_prev, c[S1])
-
-    head_a, second_a = late(edges)
-    head_b, second_b = early(edges)
-    ends = pooled(head_a + head_b, second_a + second_b)
-    pool[0, pl.ds(0, 128)] = ends[:128]
-    pool[7, pl.ds(0, 128)] = ends[128:]
-    send(up, c[PR])
+    far = first & has_prev
+    lead = second & has_next
+    send(up, "OU", own(1), own(9), above)
+    send(down, "OD", own(8), own(0), below)
+    send(lead & cross_up, "FU", own(1), old(9), (tm + 1, row - 1))
+    send(lead & cross_down, "FD", own(8), old(0), (tm + 1, row + 1))
+    send(has_next, "E0", own(1), old(1), nxt)
+    send(has_next, "E1", own(8), old(8), nxt)
+    send(has_next, "S0", own(2), old(2), nxt)
+    send(has_next, "M0", own(3, 2), old(3, 2), nxt)
+    send(has_next, "M1", own(5, 3), old(5, 3), nxt)
+
+    arrived(down, "OU", own(9))
+    send(first & down, "HU", own(9), old(9), nxt, "FU")
+    arrived(up, "OD", own(0))
+    send(first & up, "HD", own(0), old(0), nxt, "FD")
+    arrived(has_prev, "E0", old(1))
+    send(far & up & ~cross_up, "FU", old(1), old(9), above)
+    arrived(has_prev, "E1", old(8))
+    send(far & down & ~cross_down, "FD", old(8), old(0), below)
+
+    head_a, second_a = late(lambda f, b: jnp.concatenate([x[f, b], x[f, 7 + b]], axis=0))
+    z[0, 7] = head_a[128:]
+    z[1, 7] = second_a[128:]
+    arrived(up & has_prev, "FD", old(0))
+    arrived(has_prev, "S0", old(2))
+    head_b, second_b = early(lambda f, b: x[f, b])
+    top = pooled(head_a[:128] + head_b, second_a[:128] + second_b)
+    pool[0, pl.ds(0, 128)] = top
+    rim[0] = top.astype(BF16)
+    send(up, "PR", rim.at[0], rim.at[1], above)
 
     def rest_part(i, carry):
         r = 2 * i + 1
@@ -255,13 +262,17 @@
         pool[pl.ds(r, 2), pl.ds(0, 128)] = pooled(head, second).reshape(2, 128, 128)
         return carry
 
-    arrived(has_prev, c[M0])
+    arrived(has_prev, "M0", old(3, 2))
     rest_part(0, 0)
-    arrived(has_prev, c[M1])
+    arrived(has_prev, "M1", old(5, 3))
     lax.fori_loop(1, 3, rest_part, 0)
+    arrived(down & has_prev, "FU", old(9))
+    head_b, second_b = early(lambda f, b: x[f, 7 + b])
+    pool[7, pl.ds(0, 128)] = pooled(z[0, 7] + head_b, z[1, 7] + second_b)
 
     loads[2].wait()
-    arrived(down, c[PR])
+    arrived(down, "PR", rim.at[1])
+    pool[8, pl.ds(0, 128)] = rim[1].astype(F32)
     weight = wd[...].reshape(1152, 256)
     strips = [
         jnp.concatenate(
@@ -278,16 +289,19 @@
         dot(jnp.concatenate(strips, axis=0), weight).astype(BF16).reshape(4, 64, 256)
     )
 
-    send(up, c[T2U])
-    send(down, c[T2D])
-    send(has_next, c[N1A])
-    send(hop2, far_a)
-    send(has_next, c[N1B])
-    send(hop2, far_b)
-
-    loads[3].wait()
-    arrived(down, c[T2U])
-    arrived(up, c[T2D])
+    send(up, "T2U", part(2, 1), part(2, 5), above)
+    send(down, "T2D", part(2, 4), part(2, 0), below)
+    send(lead & cross_up, "T1U", part(2, 1), part(1, 5), (tm + 1, row - 1))
+    send(lead & cross_down, "T1D", part(2, 4), part(1, 0), (tm + 1, row + 1))
+    hop2 = first & has_next2
+    send(hop2 & cross_up, "T0U", part(2, 1), part(0, 5), (tm + 2, row - 1))
+    send(hop2 & cross_down, "T0D", part(2, 4), part(0, 0), (tm + 2, row + 1))
+    send(has_next, "NU", part(2, 1), part(1, 1), nxt)
+    send(has_next, "ND", part(2, 4), part(1, 4), nxt)
+    send(hop2, "QU", part(2, 1), part(0, 1), nx2)
+    send(hop2, "QD", part(2, 4), part(0, 4), nx2)
+    send(has_next, "NM", part(2, 2, 2), part(1, 2, 2), nxt)
+    send(hop2, "QM", part(2, 2, 2), part(0, 2, 2), nx2)
 
     def coarse(a, e):
         left = jnp.concatenate(
@@ -296,26 +310,36 @@
         right = jnp.concatenate([wc[a, b, pl.ds(e * 256, 256), :] for b in range(3)], axis=0)
         return dot(left, right)
 
+    loads[3].wait()
+    arrived(down, "T2U", part(2, 5))
+    send(first & down, "K1U", part(2, 5), part(1, 5), nxt, "T1U")
+    arrived(up, "T2D", part(2, 0))
+    send(first & up, "K1D", part(2, 0), part(1, 0), nxt, "T1D")
     for e in range(3):
         y[e] = coarse(2, e)
 
-    hand = first & has_prev
-    arrived(has_prev, c[N1A])
-    send(hand, hand_a)
-    send(up & has_prev, c[T1U])
-    arrived(has_prev, c[N1B])
-    send(hand, hand_b)
-    send(down & has_prev, c[T1D])
-    arrived(has_prev2, far_a)
-    send(up & has_prev2, c[T0U])
-    arrived(has_prev2, far_b)
-    send(down & has_prev2, c[T0D])
-    arrived(down & has_prev, c[T1U])
-    arrived(up & has_prev, c[T1D])
+    far2 = first & has_prev2
+    arrived(has_prev, "NU", part(1, 1))
+    send(far & up & ~cross_up, "T1U", part(1, 1), part(1, 5), above)
+    send(far, "GU", part(1, 1), part(0, 1), nxt, "QU")
+    arrived(has_prev, "ND", part(1, 4))
+    send(far & down & ~cross_down, "T1D", part(1, 4), part(1, 0), below)
+    send(far, "GD", part(1, 4), part(0, 4), nxt, "QD")
+    arrived(has_prev2, "QU", part(0, 1))
+    send(far2 & up & ~cross_up, "T0U", part(0, 1), part(0, 5), above)
+    arrived(has_prev2, "QD", part(0, 4))
+    send(far2 & down & ~cross_down, "T0D", part(0, 4), part(0, 0), below)
+    arrived(has_prev, "NM", part(1, 2, 2))
+    send(far, "GM", part(1, 2, 2), part(0, 2, 2), nxt, "QM")
+    arrived(down & has_prev, "T1U", part(1, 5))
+    send(far & down, "K0U", part(1, 5), part(0, 5), nxt, "T0U")
+    arrived(up & has_prev, "T1D", part(1, 0))
+    send(far & up, "K0D", part(1, 0), part(0, 0), nxt, "T0D")
     for e in range(3):
         y[e] = y[e] + coarse(1, e)
-    arrived(down & has_prev2, c[T0U])
-    arrived(up & has_prev2, c[T0D])
+    arrived(has_prev2, "QM", part(0, 2, 2))
+    arrived(down & has_prev2, "T0U", part(0, 5))
+    arrived(up & has_prev2, "T0D", part(0, 0))
     parts = [y[e] + coarse(0, e) for e in range(3)]
     out[...] = silu(spread(*parts, 64)).astype(BF16).reshape(1, 4, 64, 256)
 
@@ -345,10 +369,11 @@
                 pltpu.VMEM((3, 3, 768, 256), BF16),
                 pltpu.VMEM((2, 8, 128, 128), F32),
                 pltpu.VMEM((9, 136, 128), F32),
+                pltpu.VMEM((2, 128, 128), BF16),
                 pltpu.VMEM((3, 6, 64, 256), BF16),
                 pltpu.VMEM((3, 256, 256), F32),
-                pltpu.SemaphoreType.DMA((COPIES,)),
-                pltpu.SemaphoreType.DMA((COPIES,)),
+                pltpu.SemaphoreType.DMA((len(IDS),)),
+                pltpu.SemaphoreType.DMA((len(IDS),)),
                 pltpu.SemaphoreType.DMA((4,)),
             ],
             compiler_params=pltpu.CompilerParams(

time: 37 us -> 33.8 us (0.914)
  the two profiles are of different devices: /device:TPU:162 before, /device:TPU:111 now
where the time goes in v2:
time: 33.8 us; the launch traced here: 33.7 us
  Pallas kernels  32.2 us (95%)
  local copies, waits for them, and re-layouts  1.57 us (5%)
    pallas_call x1, Pallas kernels, local(): pl.pallas_call(functools.partial(kernel, tms, rws), out_shape=jax.ShapeDt...  32.2 us
    unnamed x1, local copies, waits for them, and re-layouts  1.57 us

profile of v2, /device:TPU:111, one launch (start us, length us, event | category | flops | bytes accessed | tf_op | source)
XLA Modules:
  0.0 33.7 jit_solution(18062613087270190210)
XLA Ops:
  0.0 32.2 %encoder.1 = bf16[1,4,64,256]{3,2,1,0:T(8,128)(2,1)} custom-call(bf16[2,8,128,128]{3,2,1,0:T(8,128)(2,1)} %frames.1, bf16[3,3,384,128]{3,2,1,0:T(8,128)(2,1)} %wf_h.1, bf16[3,384,256]{2,1,0:T(8,128)(2,1)} %wd_h.1, bf16[3,3,768,256]{3,2,1,0:T(8,128)(2,1)} %wc_h.1), custom_call_target="tpu_custom_call" | custom-call | tf_op jit(solution)/shard_map/encoder/pallas_call | solution.py:360
  32.2 1.6 %copy.6 = bf16[1,4,64,256]{3,2,1,0:T(8,128)(2,1)} copy(bf16[1,4,64,256]{3,2,1,0:T(8,128)(2,1)} %encoder.1) | data formatting | bytes 262144

commit v3 on v2

--- a/solution.py
+++ b/solution.py
@@ -11,8 +11,8 @@
 
 NAMES = (
     "E0", "E1", "S0", "M0", "M1", "OU", "OD", "FU", "FD", "HU", "HD", "PR",
-    "NU", "ND", "NM", "QU", "QD", "QM", "GU", "GD", "GM", "T2U", "T2D", "T1U",
-    "T1D", "T0U", "T0D", "K1U", "K1D", "K0U", "K0D",
+    "N0", "N1", "N2", "N3", "Q0", "Q1", "Q2", "Q3", "G0", "G1", "G2", "G3",
+    "T2U", "T2D", "T1U", "T1D", "T0U", "T0D", "K0U", "K0D",
 )
 IDS = {name: i for i, name in enumerate(NAMES)}
 
@@ -33,7 +33,7 @@
 
 
 def kernel(
-    tms, rws, frames, wf_h, wd_h, wc_h, out, x, wf, wd, wc, z, pool, rim, red, y, ssem, rsem, lsem
+    tms, rws, frames, wf_h, wd_h, wc_h, out, x, wf, wd, wc, z, pool, rim, red, y, ssem, rsem, lsem, near
 ):
     tm = lax.axis_index("tm")
     row = lax.axis_index("rows")
@@ -58,10 +58,6 @@
         (second & has_next & cross_down, (tm + 1, row + 1)),
         (first & has_prev & cross_up, (tm - 1, row - 1)),
         (first & has_prev & cross_down, (tm - 1, row + 1)),
-        (first & has_next2 & cross_up, (tm + 2, row - 1)),
-        (first & has_next2 & cross_down, (tm + 2, row + 1)),
-        (first & has_prev2 & cross_up, (tm - 2, row - 1)),
-        (first & has_prev2 & cross_down, (tm - 2, row + 1)),
     ):
 
         @pl.when(ok)
@@ -137,6 +133,15 @@
 
         sent.append((ok, copy))
 
+    def left(ok):
+        for i, (was, copy) in enumerate(sent):
+
+            @pl.when(was & ok)
+            def _():
+                copy.wait_send()
+
+            sent[i] = (was & ~ok, copy)
+
     def arrived(ok, name, dst):
         copy = pltpu.make_async_remote_copy(
             src_ref=dst,
@@ -222,14 +227,23 @@
     lax.fori_loop(0, 3, own_part, 0)
     pl.semaphore_wait(barrier, total)
 
+    @pl.when(has_prev)
+    def _():
+        pl.semaphore_signal(near, inc=1, device_id=(tm - 1, row), device_id_type=MESH)
+
+    @pl.when(first & has_prev2)
+    def _():
+        pl.semaphore_signal(near, inc=1, device_id=(tm - 2, row), device_id_type=MESH)
+
     far = first & has_prev
     lead = second & has_next
     send(up, "OU", own(1), own(9), above)
     send(down, "OD", own(8), own(0), below)
     send(lead & cross_up, "FU", own(1), old(9), (tm + 1, row - 1))
     send(lead & cross_down, "FD", own(8), old(0), (tm + 1, row + 1))
+    left(lead & (cross_up | cross_down))
+    send(has_next, "E1", own(8), old(8), nxt)
     send(has_next, "E0", own(1), old(1), nxt)
-    send(has_next, "E1", own(8), old(8), nxt)
     send(has_next, "S0", own(2), old(2), nxt)
     send(has_next, "M0", own(3, 2), old(3, 2), nxt)
     send(has_next, "M1", own(5, 3), old(5, 3), nxt)
@@ -238,10 +252,10 @@
     send(first & down, "HU", own(9), old(9), nxt, "FU")
     arrived(up, "OD", own(0))
     send(first & up, "HD", own(0), old(0), nxt, "FD")
+    arrived(has_prev, "E1", old(8))
+    send(far & down & ~cross_down, "FD", old(8), old(0), below)
     arrived(has_prev, "E0", old(1))
     send(far & up & ~cross_up, "FU", old(1), old(9), above)
-    arrived(has_prev, "E1", old(8))
-    send(far & down & ~cross_down, "FD", old(8), old(0), below)
 
     head_a, second_a = late(lambda f, b: jnp.concatenate([x[f, b], x[f, 7 + b]], axis=0))
     z[0, 7] = head_a[128:]
@@ -262,46 +276,56 @@
         pool[pl.ds(r, 2), pl.ds(0, 128)] = pooled(head, second).reshape(2, 128, 128)
         return carry
 
+    def reduce(p):
+        strip = [
+            pool[2 * p + b, pl.ds(e, 64, stride=2), :].astype(BF16)
+            for b in range(3)
+            for e in range(3)
+        ]
+        red[2, p + 1] = dot(jnp.concatenate(strip, axis=1), wd[...].reshape(1152, 256)).astype(BF16)
+
+    hop2 = first & has_next2
+
+    def pass_on(p):
+        send(has_next, "N%d" % p, part(2, p + 1), part(1, p + 1), nxt)
+        send(hop2, "Q%d" % p, part(2, p + 1), part(0, p + 1), nx2)
+
+    def rim_up():
+        send(up, "T2U", part(2, 1), part(2, 5), above)
+        send(up & has_next, "T1U", part(2, 1), part(1, 5), (tm + 1, row - 1))
+        send(up & hop2, "T0U", part(2, 1), part(0, 5), (tm + 2, row - 1))
+
+    def rim_down():
+        send(down, "T2D", part(2, 4), part(2, 0), below)
+        send(down & has_next, "T1D", part(2, 4), part(1, 0), (tm + 1, row + 1))
+        send(down & hop2, "T0D", part(2, 4), part(0, 0), (tm + 2, row + 1))
+
+    loads[2].wait()
+
+    @pl.when(has_next)
+    def _():
+        pl.semaphore_wait(near, 1 + hop2.astype(jnp.int32))
+
     arrived(has_prev, "M0", old(3, 2))
     rest_part(0, 0)
+    reduce(0)
+    rim_up()
+    pass_on(0)
     arrived(has_prev, "M1", old(5, 3))
-    lax.fori_loop(1, 3, rest_part, 0)
+    rest_part(1, 0)
+    reduce(1)
+    pass_on(1)
+    rest_part(2, 0)
+    reduce(2)
+    pass_on(2)
     arrived(down & has_prev, "FU", old(9))
     head_b, second_b = early(lambda f, b: x[f, 7 + b])
     pool[7, pl.ds(0, 128)] = pooled(z[0, 7] + head_b, z[1, 7] + second_b)
-
-    loads[2].wait()
     arrived(down, "PR", rim.at[1])
     pool[8, pl.ds(0, 128)] = rim[1].astype(F32)
-    weight = wd[...].reshape(1152, 256)
-    strips = [
-        jnp.concatenate(
-            [
-                pool[2 * p + b, pl.ds(e, 64, stride=2), :].astype(BF16)
-                for b in range(3)
-                for e in range(3)
-            ],
-            axis=1,
-        )
-        for p in range(4)
-    ]
-    red[2, pl.ds(1, 4)] = (
-        dot(jnp.concatenate(strips, axis=0), weight).astype(BF16).reshape(4, 64, 256)
-    )
-
-    send(up, "T2U", part(2, 1), part(2, 5), above)
-    send(down, "T2D", part(2, 4), part(2, 0), below)
-    send(lead & cross_up, "T1U", part(2, 1), part(1, 5), (tm + 1, row - 1))
-    send(lead & cross_down, "T1D", part(2, 4), part(1, 0), (tm + 1, row + 1))
-    hop2 = first & has_next2
-    send(hop2 & cross_up, "T0U", part(2, 1), part(0, 5), (tm + 2, row - 1))
-    send(hop2 & cross_down, "T0D", part(2, 4), part(0, 0), (tm + 2, row + 1))
-    send(has_next, "NU", part(2, 1), part(1, 1), nxt)
-    send(has_next, "ND", part(2, 4), part(1, 4), nxt)
-    send(hop2, "QU", part(2, 1), part(0, 1), nx2)
-    send(hop2, "QD", part(2, 4), part(0, 4), nx2)
-    send(has_next, "NM", part(2, 2, 2), part(1, 2, 2), nxt)
-    send(hop2, "QM", part(2, 2, 2), part(0, 2, 2), nx2)
+    reduce(3)
+    rim_down()
+    pass_on(3)
 
     def coarse(a, e):
         left = jnp.concatenate(
@@ -311,33 +335,23 @@
         return dot(left, right)
 
     loads[3].wait()
+    for p in range(3):
+        arrived(has_prev, "N%d" % p, part(1, p + 1))
+        send(far, "G%d" % p, part(1, p + 1), part(0, p + 1), nxt, "Q%d" % p)
+    arrived(down & has_prev, "T1U", part(1, 5))
+    send(far & down, "K0U", part(1, 5), part(0, 5), nxt, "T0U")
     arrived(down, "T2U", part(2, 5))
-    send(first & down, "K1U", part(2, 5), part(1, 5), nxt, "T1U")
     arrived(up, "T2D", part(2, 0))
-    send(first & up, "K1D", part(2, 0), part(1, 0), nxt, "T1D")
     for e in range(3):
         y[e] = coarse(2, e)
-
-    far2 = first & has_prev2
-    arrived(has_prev, "NU", part(1, 1))
-    send(far & up & ~cross_up, "T1U", part(1, 1), part(1, 5), above)
-    send(far, "GU", part(1, 1), part(0, 1), nxt, "QU")
-    arrived(has_prev, "ND", part(1, 4))
-    send(far & down & ~cross_down, "T1D", part(1, 4), part(1, 0), below)
-    send(far, "GD", part(1, 4), part(0, 4), nxt, "QD")
-    arrived(has_prev2, "QU", part(0, 1))
-    send(far2 & up & ~cross_up, "T0U", part(0, 1), part(0, 5), above)
-    arrived(has_prev2, "QD", part(0, 4))
-    send(far2 & down & ~cross_down, "T0D", part(0, 4), part(0, 0), below)
-    arrived(has_prev, "NM", part(1, 2, 2))
-    send(far, "GM", part(1, 2, 2), part(0, 2, 2), nxt, "QM")
-    arrived(down & has_prev, "T1U", part(1, 5))
-    send(far & down, "K0U", part(1, 5), part(0, 5), nxt, "T0U")
+    arrived(has_prev, "N3", part(1, 4))
+    send(far, "G3", part(1, 4), part(0, 4), nxt, "Q3")
     arrived(up & has_prev, "T1D", part(1, 0))
     send(far & up, "K0D", part(1, 0), part(0, 0), nxt, "T0D")
     for e in range(3):
         y[e] = y[e] + coarse(1, e)
-    arrived(has_prev2, "QM", part(0, 2, 2))
+    for p in range(4):
+        arrived(has_prev2, "Q%d" % p, part(0, p + 1))
     arrived(down & has_prev2, "T0U", part(0, 5))
     arrived(up & has_prev2, "T0D", part(0, 0))
     parts = [y[e] + coarse(0, e) for e in range(3)]
@@ -375,6 +389,7 @@
                 pltpu.SemaphoreType.DMA((len(IDS),)),
                 pltpu.SemaphoreType.DMA((len(IDS),)),
                 pltpu.SemaphoreType.DMA((4,)),
+                pltpu.SemaphoreType.REGULAR,
             ],
             compiler_params=pltpu.CompilerParams(
                 collective_id=0, has_side_effects=True, vmem_limit_bytes=60 * 1024 * 1024

time: 33.8 us -> 34.1 us (level)
  the two profiles are of different devices: /device:TPU:111 before, /device:TPU:7 now
where the time goes in v3:
time: 34.1 us; the launch traced here: 34 us
  Pallas kernels  32.4 us (95%)
  local copies, waits for them, and re-layouts  1.57 us (5%)
    pallas_call x1, Pallas kernels, local(): pl.pallas_call(functools.partial(kernel, tms, rws), out_shape=jax.ShapeDt...  32.4 us
    unnamed x1, local copies, waits for them, and re-layouts  1.57 us

profile of v3, /device:TPU:7, one launch (start us, length us, event | category | flops | bytes accessed | tf_op | source)
XLA Modules:
  0.0 34.0 jit_solution(17984507659733118293)
XLA Ops:
  0.0 32.4 %encoder.1 = bf16[1,4,64,256]{3,2,1,0:T(8,128)(2,1)} custom-call(bf16[2,8,128,128]{3,2,1,0:T(8,128)(2,1)} %frames.1, bf16[3,3,384,128]{3,2,1,0:T(8,128)(2,1)} %wf_h.1, bf16[3,384,256]{2,1,0:T(8,128)(2,1)} %wd_h.1, bf16[3,3,768,256]{3,2,1,0:T(8,128)(2,1)} %wc_h.1), custom_call_target="tpu_custom_call" | custom-call | tf_op jit(solution)/shard_map/encoder/pallas_call | solution.py:374
  32.4 1.6 %copy.6 = bf16[1,4,64,256]{3,2,1,0:T(8,128)(2,1)} copy(bf16[1,4,64,256]{3,2,1,0:T(8,128)(2,1)} %encoder.1) | data formatting | bytes 262144

commit v4 on v3

--- a/solution.py
+++ b/solution.py
@@ -54,10 +54,6 @@
         (down, (tm, row + 1)),
         (first & has_next2, (tm + 2, row)),
         (first & has_prev2, (tm - 2, row)),
-        (second & has_next & cross_up, (tm + 1, row - 1)),
-        (second & has_next & cross_down, (tm + 1, row + 1)),
-        (first & has_prev & cross_up, (tm - 1, row - 1)),
-        (first & has_prev & cross_down, (tm - 1, row + 1)),
     ):
 
         @pl.when(ok)
@@ -133,15 +129,6 @@
 
         sent.append((ok, copy))
 
-    def left(ok):
-        for i, (was, copy) in enumerate(sent):
-
-            @pl.when(was & ok)
-            def _():
-                copy.wait_send()
-
-            sent[i] = (was & ~ok, copy)
-
     def arrived(ok, name, dst):
         copy = pltpu.make_async_remote_copy(
             src_ref=dst,
@@ -239,18 +226,22 @@
     lead = second & has_next
     send(up, "OU", own(1), own(9), above)
     send(down, "OD", own(8), own(0), below)
-    send(lead & cross_up, "FU", own(1), old(9), (tm + 1, row - 1))
-    send(lead & cross_down, "FD", own(8), old(0), (tm + 1, row + 1))
-    left(lead & (cross_up | cross_down))
+    hold = second & ((tm // 2) % 2 == 1)
+    arrived(hold & cross_down, "OU", own(9))
+    arrived(hold & cross_up, "OD", own(0))
     send(has_next, "E1", own(8), old(8), nxt)
     send(has_next, "E0", own(1), old(1), nxt)
     send(has_next, "S0", own(2), old(2), nxt)
     send(has_next, "M0", own(3, 2), old(3, 2), nxt)
+    arrived(second & ~hold & cross_down, "OU", own(9))
+    arrived(second & ~hold & cross_up, "OD", own(0))
+    send(lead & cross_down, "HU", own(9), old(9), nxt, "FU")
+    send(lead & cross_up, "HD", own(0), old(0), nxt, "FD")
     send(has_next, "M1", own(5, 3), old(5, 3), nxt)
 
-    arrived(down, "OU", own(9))
+    arrived(down & ~(second & cross_down), "OU", own(9))
     send(first & down, "HU", own(9), old(9), nxt, "FU")
-    arrived(up, "OD", own(0))
+    arrived(up & ~(second & cross_up), "OD", own(0))
     send(first & up, "HD", own(0), old(0), nxt, "FD")
     arrived(has_prev, "E1", old(8))
     send(far & down & ~cross_down, "FD", old(8), old(0), below)

time: 34.1 us -> 31.2 us (0.915)
  the two profiles are of different devices: /device:TPU:7 before, /device:TPU:199 now
where the time goes in v4:
time: 31.2 us; the launch traced here: 31.1 us
  Pallas kernels  29.5 us (95%)
  local copies, waits for them, and re-layouts  1.57 us (5%)
    pallas_call x1, Pallas kernels, local(): pl.pallas_call(functools.partial(kernel, tms, rws), out_shape=jax.ShapeDt...  29.5 us
    unnamed x1, local copies, waits for them, and re-layouts  1.57 us

profile of v4, /device:TPU:199, one launch (start us, length us, event | category | flops | bytes accessed | tf_op | source)
XLA Modules:
  0.0 31.1 jit_solution(10316452382190920595)
XLA Ops:
  0.0 29.5 %encoder.1 = bf16[1,4,64,256]{3,2,1,0:T(8,128)(2,1)} custom-call(bf16[2,8,128,128]{3,2,1,0:T(8,128)(2,1)} %frames.1, bf16[3,3,384,128]{3,2,1,0:T(8,128)(2,1)} %wf_h.1, bf16[3,384,256]{2,1,0:T(8,128)(2,1)} %wd_h.1, bf16[3,3,768,256]{3,2,1,0:T(8,128)(2,1)} %wc_h.1), custom_call_target="tpu_custom_call" | custom-call | tf_op jit(solution)/shard_map/encoder/pallas_call | solution.py:365
  29.5 1.6 %copy.6 = bf16[1,4,64,256]{3,2,1,0:T(8,128)(2,1)} copy(bf16[1,4,64,256]{3,2,1,0:T(8,128)(2,1)} %encoder.1) | data formatting | bytes 262144

commit v5 on v4

--- a/solution.py
+++ b/solution.py
@@ -318,12 +318,19 @@
     rim_down()
     pass_on(3)
 
+    def tile(a, b, e):
+        return wc[a, b, pl.ds(e * 256, 256), :]
+
     def coarse(a, e):
-        left = jnp.concatenate(
-            [red[a, pl.ds(b, 4)].reshape(256, 256) for b in range(3)], axis=1
-        )
-        right = jnp.concatenate([wc[a, b, pl.ds(e * 256, 256), :] for b in range(3)], axis=0)
-        return dot(left, right)
+        none = jnp.zeros((64, 256), BF16)
+        r1, r2, r3, r5 = (red[a, r] for r in (1, 2, 3, 5))
+        stacks = ((none, r1, r2, r3), (r1, r2, r3, none), (r2, r3, none, r5))
+        left = jnp.concatenate([jnp.concatenate(rows, axis=0) for rows in stacks], axis=1)
+        return dot(left, jnp.concatenate([tile(a, b, e) for b in range(3)], axis=0))
+
+    def last(r, b, e):
+        left = jnp.concatenate([red[a, r] for a in range(3)], axis=1)
+        return dot(left, jnp.concatenate([tile(a, b, e) for a in range(3)], axis=0))
 
     loads[3].wait()
     for p in range(3):
@@ -332,20 +339,32 @@
     arrived(down & has_prev, "T1U", part(1, 5))
     send(far & down, "K0U", part(1, 5), part(0, 5), nxt, "T0U")
     arrived(down, "T2U", part(2, 5))
-    arrived(up, "T2D", part(2, 0))
     for e in range(3):
-        y[e] = coarse(2, e)
+        y[e] = coarse(2, e) + coarse(1, e)
+    for p in range(3):
+        arrived(has_prev2, "Q%d" % p, part(0, p + 1))
+    arrived(down & has_prev2, "T0U", part(0, 5))
+    for e in range(3):
+        y[e] = y[e] + coarse(0, e)
     arrived(has_prev, "N3", part(1, 4))
     send(far, "G3", part(1, 4), part(0, 4), nxt, "Q3")
     arrived(up & has_prev, "T1D", part(1, 0))
     send(far & up, "K0D", part(1, 0), part(0, 0), nxt, "T0D")
-    for e in range(3):
-        y[e] = y[e] + coarse(1, e)
-    for p in range(4):
-        arrived(has_prev2, "Q%d" % p, part(0, p + 1))
-    arrived(down & has_prev2, "T0U", part(0, 5))
+    arrived(up, "T2D", part(2, 0))
+    arrived(has_prev2, "Q3", part(0, 4))
     arrived(up & has_prev2, "T0D", part(0, 0))
-    parts = [y[e] + coarse(0, e) for e in range(3)]
+    parts = [
+        jnp.concatenate(
+            [
+                y[e, pl.ds(0, 64)] + last(0, 0, e),
+                y[e, pl.ds(64, 64)],
+                y[e, pl.ds(128, 64)] + last(4, 2, e),
+                y[e, pl.ds(192, 64)] + last(4, 1, e),
+            ],
+            axis=0,
+        )
+        for e in range(3)
+    ]
     out[...] = silu(spread(*parts, 64)).astype(BF16).reshape(1, 4, 64, 256)
 
     for ok, copy in sent:
@@ -383,7 +402,7 @@
                 pltpu.SemaphoreType.REGULAR,
             ],
             compiler_params=pltpu.CompilerParams(
-                collective_id=0, has_side_effects=True, vmem_limit_bytes=60 * 1024 * 1024
+                collective_id=0, has_side_effects=True, vmem_limit_bytes=54800 * 1024
             ),
             name="encoder",
         )(frames, conv_fine, conv_down, conv_coarse)

time: 31.2 us -> 29.1 us (0.933)
  the two profiles are of different devices: /device:TPU:199 before, /device:TPU:162 now
where the time goes in v5:
time: 29.1 us; the launch traced here: 28.9 us
  Pallas kernels  28.3 us (97%)
  local copies, waits for them, and re-layouts  0.66 us (2%)
    pallas_call x1, Pallas kernels, local(): pl.pallas_call(functools.partial(kernel, tms, rws), out_shape=jax.ShapeDt...  28.3 us
    unnamed x1, local copies, waits for them, and re-layouts  0.66 us

profile of v5, /device:TPU:162, one launch (start us, length us, event | category | flops | bytes accessed | tf_op | source)
XLA Modules:
  0.0 28.9 jit_solution(12881150021144811214)
XLA Ops:
  0.0 28.3 %encoder.1 = bf16[1,4,64,256]{3,2,1,0:T(8,128)(2,1)S(1)} custom-call(bf16[2,8,128,128]{3,2,1,0:T(8,128)(2,1)} %frames.1, bf16[3,3,384,128]{3,2,1,0:T(8,128)(2,1)} %wf_h.1, bf16[3,384,256]{2,1,0:T(8,128)(2,1)} %wd_h.1, bf16[3,3,768,256]{3,2,1,0:T(8,128)(2,1)} %wc_h.1), custom_call_target="tpu_custom_call" | custom-call | tf_op jit(solution)/shard_map/encoder/pallas_call | solution.py:384
  28.3 0.7 %copy.6 = bf16[1,4,64,256]{3,2,1,0:T(8,128)(2,1)} copy(bf16[1,4,64,256]{3,2,1,0:T(8,128)(2,1)S(1)} %encoder.1) | data formatting | bytes 262144
